TPU v7x, 32 devices: a 4x4x1 block of a 4x4x8 slice. The times are simulated.
32 devices in a mesh: dp: 1 (over z), cy: 4 (over y), cx: 4 (over x), core: 2 (over core).
Axes of the slice: x: 4, y: 4, z: 1, core: 2. Of those that a mesh axis runs over, the one named last changes fastest.
The devices are a block of a 4x4x8 slice.
Arguments:
- x_in: bfloat16 [1, 3072, 2048], P('dp', ('cy', 'cx', 'core'))
- w_qkv: bfloat16 [2048, 32, 128], replicated
- w_out: bfloat16 [16, 128, 2048], replicated
Outputs:
- output: bfloat16 [1, 3072, 2048], P('dp', ('cy', 'cx', 'core'))
All inputs are finite; a program needn't handle non-finite values.
Results may differ from a plain program's by a relative error of at most 0.00801081.
Values are sent between devices in bfloat16 or wider.
A program may use at most 768 MiB of HBM per device.

v0:
```python
import jax
import jax.numpy as jnp
from jax import lax
from jax.sharding import PartitionSpec as P


def solution(mesh):
    cy_size = mesh.shape["cy"]
    head_split = mesh.shape["cx"] * mesh.shape["core"]
    seq_spec = P("dp", ("cy", "cx", "core"))

    def local_layer(x_loc, w_qkv, w_out):
        num_heads = w_out.shape[0]
        head_dim = w_out.shape[1]
        num_kv = (w_qkv.shape[1] - num_heads) // 2
        num_tokens = x_loc.shape[1]
        kv_slots = max(num_kv, head_split)
        repeat_kv = kv_slots // num_kv
        q_local = num_heads // head_split
        kv_local = kv_slots // head_split
        group_size = q_local // kv_local
        qkv_rows = jnp.einsum("sc,chd->shd", x_loc[0], w_qkv, preferred_element_type=jnp.float32).astype(jnp.bfloat16)
        q_part = qkv_rows[:, :num_heads].reshape(num_tokens, head_split, q_local, head_dim)
        k_part = jnp.repeat(qkv_rows[:, num_heads:num_heads + num_kv], repeat_kv, axis=1).reshape(num_tokens, head_split, kv_local, head_dim)
        v_part = jnp.repeat(qkv_rows[:, num_heads + num_kv:], repeat_kv, axis=1).reshape(num_tokens, head_split, kv_local, head_dim)
        packed = jnp.concatenate([q_part, k_part, v_part], axis=2)
        packed = lax.all_to_all(packed, "cx", 1, 0, tiled=True)
        packed = lax.all_to_all(packed, "core", 1, 0, tiled=True)
        seq_len = packed.shape[0]
        queries = packed[:, 0, :q_local].reshape(seq_len, kv_local, group_size, head_dim)
        kv_all = lax.all_gather(packed[:, 0, q_local:], "cy")
        logit_scale = head_dim ** -0.5
        run_max = jnp.full((kv_local, group_size, seq_len), -jnp.inf, jnp.float32)
        run_sum = jnp.zeros((kv_local, group_size, seq_len), jnp.float32)
        accumulator = jnp.zeros((kv_local, group_size, seq_len, head_dim), jnp.float32)
        for block_idx in range(cy_size):
            k_block = kv_all[block_idx, :, :kv_local]
            v_block = kv_all[block_idx, :, kv_local:]
            scores = jnp.einsum("qkgd,skd->kgqs", queries, k_block, preferred_element_type=jnp.float32) * logit_scale
            new_max = jnp.maximum(run_max, scores.max(axis=-1))
            rescale = jnp.exp(run_max - new_max)
            weights = jnp.exp(scores - new_max[..., None])
            run_sum = run_sum * rescale + weights.sum(axis=-1)
            accumulator = accumulator * rescale[..., None] + jnp.einsum("kgqs,skd->kgqd", weights.astype(jnp.bfloat16), v_block, preferred_element_type=jnp.float32)
            run_max = new_max
        attn_out = (accumulator / run_sum[..., None]).astype(jnp.bfloat16)
        attn_out = jnp.transpose(attn_out, (2, 0, 1, 3)).reshape(seq_len, q_local, head_dim)
        attn_out = lax.all_to_all(attn_out, "core", 0, 1, tiled=True)
        attn_out = lax.all_to_all(attn_out, "cx", 0, 1, tiled=True)
        y_local = jnp.einsum("shd,hdc->sc", attn_out, w_out, preferred_element_type=jnp.float32)
        return y_local.astype(jnp.bfloat16)[None]

    return jax.shard_map(local_layer, mesh=mesh, in_specs=(seq_spec, P(), P()), out_specs=seq_spec, check_vma=False)
```

profile of v0, /device:TPU:97, one launch (start us, length us, event | category | flops | bytes accessed | tf_op | source)
XLA Modules:
  0.0 104.4 jit_solution(7914486766679727987)
XLA Ops:
  6.5 0.0 copy-start
  6.6 0.0 all-gather.3.cloned.1.call-start
  6.6 1.0 copy-done
  7.5 11.3 %fusion.36 = bf16[96,32,128]{2,0,1:T(8,128)(2,1)S(1)} fusion(bf16[2048,32,128]{2,1,0:T(8,128)(2,1)} %param.4, bf16[1,96,2048]{2,1,0:T(8,128)(2,1)S(1)} %copy-done), kind=kOutput, calls=%fused_computation.41 | convolution fusion | flops 1611005952 | bytes 17956864 | tf_op jit(solution)/shard_map/sc,chd->shd/dot_general | solution.py:22
  19.0 0.1 pad_maximum_fusion
  19.1 16.3 %all_to_all.72 = bf16[96,8,4,128]{3,0,2,1:T(8,128)(2,1)S(1)} all-to-all(bf16[96,8,4,128]{3,0,2,1:T(8,128)(2,1)S(1)} %pad_maximum_fusion), channel_id=1, replica_groups=mesh['dp'=1,'cy'=4,'cx'=4,'core'=2] {'cx'}, dimensions={1} | all-to-all | bytes 1572864 | tf_op jit(solution)/shard_map/all_to_all | solution.py:27
  35.4 0.1 copy.62
  35.5 5.9 %all_to_all.73 = bf16[384,2,4,128]{3,0,2,1:T(8,128)(2,1)S(1)} all-to-all(bf16[384,2,4,128]{3,0,2,1:T(8,128)(2,1)S(1)} %bitcast.240), channel_id=1, replica_groups=mesh['dp'=1,'cy'=4,'cx'=4,'core'=2] {'core'}, dimensions={1} | all-to-all | bytes 1572864 | tf_op jit(solution)/shard_map/all_to_all | solution.py:28
  41.4 0.1 copy.63
  41.5 0.8 slice.55
  42.2 0.1 all-gather.3.cloned.1.call-update
  42.3 24.3 %all-gather.3.cloned.1.call-done = bf16[3072,1,2,128]{3,0,2,1:T(8,128)(2,1)} async-done(((bf16[768,1,2,128]{3,0,2,1:T(8,128)(2,1)}), bf16[3072,1,2,128]{3,0,2,1:T(8,128)(2,1)}) %all-gather.3.cloned.1.call-update) | async-done | bytes 1572880 | tf_op jit(solution)/shard_map/all_gather | solution.py:31
  66.6 0.0 copy-start.1
  66.6 1.8 %bitcast_reduce_fusion = (f32[2,768]{1,0:T(2,128)S(1)}, f32[768,768,2]{1,0,2:T(8,128)S(1)}) fusion(bf16[768,1,4,128]{3,0,2,1:T(8,128)(2,1)S(1)} %bitcast.235, bf16[4,768,2,128]{3,1,0,2:T(8,128)(2,1)} %bitcast.247), kind=kOutput, calls=%fused_computation.3 | convolution fusion | flops 304347648 | bytes 5314560 | tf_op jit(solution)/shard_map/qkgd,skd->kgqs/dot_general | solution.py:39
  68.4 0.0 copy-done.1
  68.5 0.8 bitcast_reduce_fusion.1
  69.3 0.8 bitcast_reduce_fusion.2
  70.1 0.8 bitcast_reduce_fusion.3
  70.9 0.9 fusion.15
  71.8 1.6 %fusion.6 = (f32[2,768]{1,0:T(2,128)S(1)}, f32[2,768]{1,0:T(2,128)S(1)}) fusion(f32[768,768,2]{1,0,2:T(8,128)S(1)} %get-tuple-element.20, f32[2,768]{1,0:T(2,128)S(1)} %get-tuple-element.19, f32[2,768]{1,0:T(2,128)S(1)} %get-tuple-element.9, f32[768,768,2]{1,0,2:T(8,128)S(1)} %get-tuple-element.16), kind=kLoop, calls=%fused_computation.14 | loop fusion | flops 7074816 | bytes 9461760 | tf_op jit(solution)/shard_map/reduce_sum | solution.py:43
  73.3 0.9 fusion.21
  74.3 1.6 %fusion.8 = (f32[2,768]{1,0:T(2,128)S(1)}, f32[2,768]{1,0:T(2,128)S(1)}) fusion(f32[768,768,2]{1,0,2:T(8,128)S(1)} %get-tuple-element.22, f32[2,768]{1,0:T(2,128)S(1)} %get-tuple-element.11, f32[2,768]{1,0:T(2,128)S(1)} %get-tuple-element.10, f32[768,768,2]{1,0,2:T(8,128)S(1)} %get-tuple-element.18), kind=kLoop, calls=%fused_computation.16 | loop fusion | flops 7074816 | bytes 9461760 | tf_op jit(solution)/shard_map/reduce_sum | solution.py:43
  75.9 0.0 slice-start
  75.9 1.5 %fusion.48 = f32[2,768,128]{2,1,0:T(8,128)S(1)} fusion(f32[2,768,128]{2,1,0:T(8,128)S(1)} %fusion.21, f32[768,768,2]{1,0,2:T(8,128)S(1)} %get-tuple-element.20, f32[2,768]{1,0:T(2,128)S(1)} %get-tuple-element.19, f32[2,768]{1,0:T(2,128)S(1)} %get-tuple-element.8, f32[2,768]{1,0:T(2,128)S(1)} %get-tuple-element.7, f32[2,768]{1,0:T(2,128)S(1)} %get-tuple-element.14, ...), kind=kOutput, calls=%fused_computation.45 | convolution fusion | flops 306315264 | bytes 6512640 | tf_op jit(solution)/shard_map/kgqs,skd->kgqd/dot_general | solution.py:44
  77.3 0.0 slice-start.1
  77.4 1.4 %fusion.66 = bf16[768,2,128]{2,0,1:T(8,128)(2,1)S(1)} fusion(f32[2,768,128]{2,1,0:T(8,128)S(1)} %fusion.15, f32[2,768,128]{2,1,0:T(8,128)S(1)} %fusion.48, f32[768,768,2]{1,0,2:T(8,128)S(1)} %get-tuple-element.18, f32[2,768]{1,0:T(2,128)S(1)} %get-tuple-element.10, f32[2,768]{1,0:T(2,128)S(1)} %get-tuple-element.5, f32[2,768]{1,0:T(2,128)S(1)} %get-tuple-element.6, ...), kind=kOutput, calls=%fused_computation.51 | convolution fusion | flops 306511872 | bytes 6899712 | tf_op jit(solution)/shard_map/kgqs,skd->kgqd/dot_general | solution.py:44
  78.7 0.4 copy.76
  79.1 4.6 %all_to_all.74 = bf16[768,2,128]{2,1,0:T(2,128)(2,1)S(1)} all-to-all(bf16[768,2,128]{2,1,0:T(2,128)(2,1)S(1)} %copy.76), channel_id=1, replica_groups=mesh['dp'=1,'cy'=4,'cx'=4,'core'=2] {'core'}, dimensions={0} | all-to-all | bytes 786432 | tf_op jit(solution)/shard_map/all_to_all | solution.py:48
  83.8 0.1 copy.77
  83.9 0.3 copy.79
  84.2 11.0 %all_to_all.75 = bf16[384,4,128]{2,1,0:T(4,128)(2,1)S(1)} all-to-all(bf16[384,4,128]{2,1,0:T(4,128)(2,1)S(1)} %copy.79), channel_id=1, replica_groups=mesh['dp'=1,'cy'=4,'cx'=4,'core'=2] {'cx'}, dimensions={0} | all-to-all | bytes 786432 | tf_op jit(solution)/shard_map/all_to_all | solution.py:49
  95.2 0.1 copy.80
  95.3 0.0 slice-done
  95.3 0.0 slice-done.1
  95.3 2.2 %fusion.35 = bf16[1,96,2048]{2,1,0:T(8,128)(2,1)} fusion(bf16[96,16,128]{2,0,1:T(8,128)(2,1)S(1)} %bitcast.242, bf16[16,128,2048]{2,1,0:T(8,128)(2,1)S(1)} %bitcast.233), kind=kOutput, calls=%fused_computation.40 | convolution fusion | flops 805502976 | bytes 9175040 | tf_op jit(solution)/shard_map/shd,hdc->sc/dot_general | solution.py:50
  (7 shorter events, 0.2 us)
Async XLA Ops:
  6.5 1.0 copy-start
  6.6 60.1 %all-gather.3.cloned.1.call-start = ((), (), s32[]{:S(2)}) async-start(), calls=%async_computation.4 | async-start | bytes 1966080 | tf_op jit(solution)/shard_map/all_gather | solution.py:31
  66.6 1.8 %copy-start.1 = (bf16[3072,1,2,128]{3,0,2,1:T(8,128)(2,1)S(1)}, bf16[3072,1,2,128]{3,0,2,1:T(8,128)(2,1)}, u32[]{:S(2)}) copy-start(bf16[3072,1,2,128]{3,0,2,1:T(8,128)(2,1)} %all-gather.3.cloned.1.call-done) | copy-start | bytes 4718596
  75.9 19.4 %slice-start = ((s8[8388608]{0:T(1024)(128)(4,1)}), s8[4194304]{0:T(1024)(128)(4,1)S(1)}, s32[]{:S(2)}) async-start(s8[8388608]{0:T(1024)(128)(4,1)} %bitcast.232), calls=%async_computation.5 | async-start | bytes 8388608
  77.3 17.9 %slice-start.1 = ((s8[8388608]{0:T(1024)(128)(4,1)}), s8[4194304]{0:T(1024)(128)(4,1)S(1)}, s32[]{:S(2)}) async-start(s8[8388608]{0:T(1024)(128)(4,1)} %bitcast.232), calls=%async_computation.6 | async-start | bytes 8388608
Sparse Core Ops, SparseCore 0:
  42.4 24.1 all-gather.2
where the time goes:
time: 105 us; the launch traced here: 104 us
  blocking collectives  37.9 us (36%)
  waiting for transfers between devices  24.4 us (23%)
  matrix products  22.4 us (21%)
  between operations  13.6 us (13%)
  other arithmetic  3.26 us (3%)
  local copies, waits for them, and re-layouts  2.83 us (3%)
    all_gather x1, waiting for transfers between devices, local_layer(): kv_all = lax.all_gather(packed[:, 0, q_local:], 'cy')  24.3 us
    all_to_all x1, blocking collectives, local_layer(): packed = lax.all_to_all(packed, 'cx', 1, 0, tiled=True)  16.3 us
    dot_general x1, matrix products, local_layer(): jnp.einsum('sc,chd->shd', x_loc[0], w_qkv, preferred_element_type=jnp.flo...  11.3 us
    all_to_all x1, blocking collectives, local_layer(): attn_out = lax.all_to_all(attn_out, 'cx', 0, 1, tiled=True)  11 us
    all_to_all x1, blocking collectives, local_layer(): packed = lax.all_to_all(packed, 'core', 1, 0, tiled=True)  5.95 us
    dot_general x4, matrix products, local_layer(): jnp.einsum('kgqs,skd->kgqd', weights.astype(jnp.bfloat16), v_block, prefe...  4.64 us
    all_to_all x1, blocking collectives, local_layer(): attn_out = lax.all_to_all(attn_out, 'core', 0, 1, tiled=True)  4.62 us
    dot_general x4, matrix products, local_layer(): jnp.einsum('qkgd,skd->kgqs', queries, k_block, preferred_element_type=jnp...  4.22 us
  transfers between devices with their start and end apart: 1, of which 1 were waited for; matrix products, arithmetic and copies ran while one was open for 0% of the time, Pallas kernels for 0%

commit v1 on v0

v1 whole, which is shorter than its diff:
```python
import functools
import math

import jax
import jax.numpy as jnp
from jax import lax
from jax.experimental import pallas as pl
from jax.experimental.pallas import tpu as pltpu
from jax.sharding import PartitionSpec as P

MESH = pl.DeviceIdType.MESH
F32 = jnp.float32
BF16 = jnp.bfloat16


def kernel(n, x_hbm, w_hbm, wo_hbm, y_ref,
           xbuf, xil, wstage, wn, wo, kvout, qout, kvb, qb, acc, mrun, lrun, osend, orecv,
           sem_x, sem_w, sem_wo, sx_send, sx_recv, s_kv1, r_kv1, s_q1, r_q1,
           s_kv2, r_kv2, s_kv3, r_kv3, s_o, r_o):
    dp = lax.axis_index("dp")
    cy = lax.axis_index("cy")
    cx = lax.axis_index("cx")
    c = lax.axis_index("core")
    a = cx * (1 - c) + cy * c
    b = cy * (1 - c) + cx * c
    tok = xbuf.shape[1]
    dim = kvb.shape[-1]
    chip = 2 * tok
    width = xbuf.shape[2]
    half = 4 // n

    def dev(da, db, core):
        ra = lax.rem(a + da + n, n)
        rb = lax.rem(b + db + n, n)
        return (dp, rb * (1 - c) + ra * c, ra * (1 - c) + rb * c, core)

    def remote(src, dst, ssem, rsem, device):
        return pltpu.make_async_remote_copy(
            src_ref=src, dst_ref=dst, send_sem=ssem, recv_sem=rsem, device_id=device, device_id_type=MESH)

    x_cp = pltpu.make_async_copy(x_hbm.at[0], xbuf.at[c], sem_x)
    x_cp.start()
    npair = w_hbm.shape[1]
    nq, nkv = npair // 2, npair // 4
    own = nq // 2
    pairs = []
    for i in range(own // 2):
        pairs += [nq + (own // 2) * c + i, nq + nkv + (own // 2) * c + i]
    for i in range(own):
        pairs.append(own * c + i)
    w_cps = [pltpu.make_async_copy(w_hbm.at[:, p], wstage.at[i], sem_w.at[i]) for i, p in enumerate(pairs)]
    for cp in w_cps:
        cp.start()

    barrier = pltpu.get_barrier_semaphore()
    peers = [dev(0, 0, 1 - c)]
    for d in range(1, n):
        for core in (c, 1 - c):
            peers += [dev(d, 0, core), dev(0, d, core)]
    for p in peers:
        pl.semaphore_signal(barrier, inc=1, device_id=p, device_id_type=MESH)

    def expand(core):
        er = lax.broadcasted_iota(jnp.int32, (dim, 4 * dim), 0)
        ec = lax.broadcasted_iota(jnp.int32, (dim, 4 * dim), 1)
        sel = jnp.where(ec < 2 * dim, 2 * er, 2 * dim + 2 * er + 1)
        e = jnp.where(ec == sel, 1.0, 0.0).astype(BF16)
        nb = width // dim
        r0 = pl.multiple_of(core * tok, tok)
        r1 = pl.multiple_of(chip + core * tok, tok)
        step = 4
        for j0 in range(0, nb, step):
            xs = jnp.concatenate([xbuf[core, :, (j0 + j) * dim:(j0 + j + 1) * dim] for j in range(step)], axis=0)
            r = jnp.dot(xs, e, preferred_element_type=F32).astype(BF16)
            for j in range(step):
                cols = slice((j0 + j) * 2 * dim, (j0 + j + 1) * 2 * dim)
                xil[pl.ds(r0, tok), cols] = r[j * tok:(j + 1) * tok, :2 * dim]
                xil[pl.ds(r1, tok), cols] = r[j * tok:(j + 1) * tok, 2 * dim:]

    x_cp.wait()
    pl.semaphore_wait(barrier, len(peers))
    x_rc = remote(xbuf.at[c], xbuf.at[c], sx_send, sx_recv, dev(0, 0, 1 - c))
    x_rc.start()
    expand(c)

    rows = 2 * w_hbm.shape[0]
    blk = 256
    for i in range(len(pairs)):
        w_cps[i].wait()

        def relay(t, _, i=i):
            k0 = pl.multiple_of(t * (blk // 2), blk // 2)
            r0 = pl.multiple_of(t * blk, blk)
            wn[i // 2, pl.ds(r0, blk), (i % 2) * dim:(i % 2 + 1) * dim] = \
                wstage[i, pl.ds(k0, blk // 2)].reshape(blk, dim)
            return 0

        lax.fori_loop(0, rows // blk, relay, 0)
    wo_cps = []
    for g in range(wo.shape[0]):
        cp = pltpu.make_async_copy(wo_hbm.at[g], wo.at[g], sem_wo.at[g])
        cp.start()
        wo_cps.append(cp)

    x_rc.wait_recv()
    expand(1 - c)

    for i in range(own // 2):
        r = jnp.dot(xil[...], wn[i], preferred_element_type=F32).astype(BF16)
        for e in range(2):
            for kv in range(2):
                kvout[2 * i + e, kv] = r[e * chip:(e + 1) * chip, kv * dim:(kv + 1) * dim]
    mine = pl.ds(pl.multiple_of(a * chip, chip), chip)
    sends = []
    for k, d in enumerate((2, 1, 3)):
        cp = remote(kvout.at[lax.rem(a + d, n)], kvb.at[0, :, mine], s_kv1.at[k], r_kv1.at[a], dev(d, 0, c))
        cp.start()
        sends.append(cp)

    def forward(src, piece):
        where = pl.ds(pl.multiple_of(piece * chip, chip), chip)
        for k, d in enumerate((1, -1)):
            cp = remote(src, kvb.at[1 + k, :, where], s_kv2.at[k, piece], r_kv2.at[k, piece], dev(0, d, c))
            cp.start()

    forward(kvout.at[a], a)
    for i in range(own // 2):
        r = jnp.dot(xil[...], wn[own // 2 + i], preferred_element_type=F32).astype(BF16)
        for e in range(2):
            for h in range(2):
                qout[2 * i + e, h] = r[h * chip:(h + 1) * chip, e * dim:(e + 1) * dim]
    for k, d in enumerate((2, 1, 3)):
        cp = remote(qout.at[lax.rem(a + d, n)], qb.at[:, mine], s_q1.at[k], r_q1.at[a], dev(d, 0, c))
        cp.start()
        sends.append(cp)
    kvb[0, :, mine] = kvout[a]
    qb[:, mine] = qout[a]

    def recv(dst, sem):
        remote(dst, dst, s_kv1.at[0], sem, dev(1, 0, c)).wait_recv()

    for d in (1, 3, 2):
        piece = lax.rem(a + d, n)
        where = pl.ds(pl.multiple_of(piece * chip, chip), chip)
        recv(kvb.at[0, :, where], r_kv1.at[piece])
        forward(kvb.at[0, :, where], piece)
    for d in (1, 3, 2):
        piece = lax.rem(a + d, n)
        where = pl.ds(pl.multiple_of(piece * chip, chip), chip)
        recv(qb.at[:, where], r_q1.at[piece])

    scale = dim ** -0.5 * math.log2(math.e)

    def attend(block, t, first, last):
        rows = pl.ds(pl.multiple_of(t * chip, chip), chip)
        q = qb[:, rows].reshape(2 * chip, dim)
        keys = kvb.shape[2]
        s = lax.dot_general(q, kvb[block, 0], (((1,), (1,)), ((), ())), preferred_element_type=F32)
        m_new = jnp.max(s, axis=1, keepdims=True)
        if not first:
            m_old = mrun[t][:, :1]
            m_new = jnp.maximum(m_new, m_old)
            alpha = jnp.exp2((m_old - m_new) * scale)
        p = jnp.exp2((s - m_new) * scale)
        l = p[:, :dim]
        for j in range(1, keys // dim):
            l = l + p[:, j * dim:(j + 1) * dim]
        o = jnp.dot(p.astype(BF16), kvb[block, 1], preferred_element_type=F32)
        if not first:
            l = lrun[t] * alpha + l
            o = acc[t] * alpha + o
        if last:
            o = (o / jnp.sum(l, axis=1, keepdims=True)).astype(BF16)
            osend[t] = o.reshape(2, chip, dim)
        else:
            mrun[t] = jnp.broadcast_to(m_new, (2 * chip, dim))
            lrun[t] = l
            acc[t] = o

    def attend_all(block, first):
        for t in range(n):
            attend(block, t, first, False)

    attend_all(0, True)

    def spot(p):
        return pl.ds(p * chip, chip)

    h = n // 2
    for p in range(h):
        recv(kvb.at[1, :, spot(p)], r_kv2.at[0, p])
        remote(kvb.at[1, :, spot(p)], kvb.at[3, :, spot(p)], s_kv3.at[p], r_kv3.at[p], dev(0, 1, c)).start()
    for p in range(h, n):
        recv(kvb.at[2, :, spot(p)], r_kv2.at[1, p])
        remote(kvb.at[2, :, spot(p)], kvb.at[3, :, spot(p)], s_kv3.at[p], r_kv3.at[p], dev(0, -1, c)).start()
    for p in range(h, n):
        recv(kvb.at[1, :, spot(p)], r_kv2.at[0, p])
    attend_all(1, False)
    for p in range(h):
        recv(kvb.at[2, :, spot(p)], r_kv2.at[1, p])
    attend_all(2, False)
    for p in range(n):
        recv(kvb.at[3, :, spot(p)], r_kv3.at[p])

    head = own * c + a
    for k, d in enumerate((2, 1, 3, 0)):
        t = lax.rem(a + d, n)
        attend(3, t, False, True)
        for e in range(2):
            core = c if e == 0 else 1 - c
            part = pl.ds(pl.multiple_of(core * tok, tok), tok)
            if d == 0 and e == 0:
                orecv[head] = osend[t, :, part]
            else:
                cp = remote(osend.at[t, :, part], orecv.at[head], s_o.at[k, e], r_o.at[head], dev(d, 0, core))
                cp.start()
                sends.append(cp)

    order = [(0, 0), (0, 1), (1, 0), (1, 1), (3, 0), (3, 1), (2, 0), (2, 1)]
    for cp in wo_cps:
        cp.wait()
    for k, (d, e) in enumerate(order):
        if e == 0:
            g = own * c + lax.rem(a + d, n)
        else:
            g = own * (1 - c) + lax.rem(b + d, n)
        if k > 0:
            recv(orecv.at[g], r_o.at[g])
        o = jnp.concatenate([orecv[g, 0], orecv[g, 1]], axis=1)
        r = jnp.dot(o, wo[g], preferred_element_type=F32)
        if k == 0:
            yacc = r
        else:
            yacc = yacc + r
    y_ref[0] = yacc.astype(BF16)

    x_rc.wait_send()
    for cp in sends:
        cp.wait_send()
    for p in range(n):
        for k, d in enumerate((1, -1)):
            remote(kvb.at[0, :, spot(p)], kvb.at[1 + k, :, spot(p)], s_kv2.at[k, p], r_kv2.at[k, p],
                   dev(0, d, c)).wait_send()
        remote(kvb.at[1, :, spot(p)], kvb.at[3, :, spot(p)], s_kv3.at[p], r_kv3.at[p], dev(0, 1, c)).wait_send()


def solution(mesh):
    n = mesh.shape["cx"]
    assert mesh.shape["cy"] == n and n == 4 and mesh.shape["core"] == 2
    seq_spec = P("dp", ("cy", "cx", "core"))

    def local_layer(x_loc, w_qkv, w_out):
        _, tok, width = x_loc.shape
        heads, dim, out_width = w_out.shape
        all_heads = w_qkv.shape[1]
        kv = (all_heads - heads) // 2
        assert kv == 2 * n and heads == 2 * kv
        chip = 2 * tok
        keys = n * chip
        w_pairs = w_qkv.reshape(width, all_heads // 2, 2, dim)
        wo_pairs = w_out.reshape(kv, 2 * dim, out_width)
        dma = pltpu.SemaphoreType.DMA
        return pl.pallas_call(
            functools.partial(kernel, n),
            out_shape=jax.ShapeDtypeStruct(x_loc.shape, BF16),
            in_specs=[pl.BlockSpec(memory_space=pl.ANY)] * 3,
            out_specs=pl.BlockSpec(memory_space=pltpu.VMEM),
            scratch_shapes=[
                pltpu.VMEM((2, tok, width), BF16),
                pltpu.VMEM((2 * chip, 2 * width), BF16),
                pltpu.VMEM((kv, width, 2, dim), BF16),
                pltpu.VMEM((kv // 2, 2 * width, 2 * dim), BF16),
                pltpu.VMEM((kv, 2 * dim, out_width), BF16),
                pltpu.VMEM((n, 2, chip, dim), BF16),
                pltpu.VMEM((n, 2, chip, dim), BF16),
                pltpu.VMEM((4, 2, keys, dim), BF16),
                pltpu.VMEM((2, keys, dim), BF16),
                pltpu.VMEM((n, 2 * chip, dim), F32),
                pltpu.VMEM((n, 2 * chip, dim), F32),
                pltpu.VMEM((n, 2 * chip, dim), F32),
                pltpu.VMEM((n, 2, chip, dim), BF16),
                pltpu.VMEM((kv, 2, tok, dim), BF16),
                dma, dma((kv,)), dma((kv,)),
                dma, dma,
                dma((3,)), dma((n,)), dma((3,)), dma((n,)),
                dma((2, n)), dma((2, n)), dma((n,)), dma((n,)),
                dma((n, 2)), dma((kv,)),
            ],
            compiler_params=pltpu.CompilerParams(
                collective_id=0, has_side_effects=True, vmem_limit_bytes=60 * 1024 * 1024),
        )(x_loc, w_pairs, wo_pairs)

    return jax.shard_map(local_layer, mesh=mesh, in_specs=(seq_spec, P(), P()), out_specs=seq_spec, check_vma=False)
```

time: 105 us -> 44.7 us (0.43)
  Pallas kernels: 0 us -> 42.8 us
  blocking collectives: 37.9 us -> 0 us
  waiting for transfers between devices: 24.4 us -> 0 us
  matrix products: 22.4 us -> 0 us
  between operations: 13.6 us -> 0.01 us
  other arithmetic: 3.26 us -> 0 us
  local copies, waits for them, and re-layouts: 2.83 us -> 1.77 us
    pallas_call x0 -> x1, Pallas kernels: none -> 42.8 us  [local_layer(): pl.pallas_call(functools.partial(kernel, n), out_shape=jax.ShapeDtypeStru...]
    all_to_all x4 -> x0, blocking collectives: 37.9 us -> none  [the longest x1 16.3 us: local_layer(): packed = lax.all_to_all(packed, 'cx', 1, 0, tiled=True)]
    all_gather x1 -> x0, waiting for transfers between devices: 24.3 us -> none  [local_layer(): kv_all = lax.all_gather(packed[:, 0, q_local:], 'cy')]
    dot_general x10 -> x0, matrix products: 22.4 us -> none  [the longest x1 11.3 us: local_layer(): jnp.einsum('sc,chd->shd', x_loc[0], w_qkv, preferred_element_type=jnp.flo...]
    reduce_sum x2 -> x0, other arithmetic: 3.12 us -> none  [local_layer(): run_sum = run_sum * rescale + weights.sum(axis=-1)]
  transfers between devices with their start and end apart: 1 -> 0, of which waited for: 1 -> 0; matrix products, arithmetic and copies ran while one was open for 0% -> 0% of each run, Pallas kernels for 0% -> 0%
where the time goes in v1:
time: 44.7 us; the launch traced here: 44.6 us
  Pallas kernels  42.8 us (96%)
  local copies, waits for them, and re-layouts  1.77 us (4%)
    pallas_call x1, Pallas kernels, local_layer(): pl.pallas_call(functools.partial(kernel, n), out_shape=jax.ShapeDtypeStru...  42.8 us
    unnamed x1, local copies, waits for them, and re-layouts  1.77 us

profile of v1, /device:TPU:97, one launch (start us, length us, event | category | flops | bytes accessed | tf_op | source)
XLA Modules:
  0.0 44.6 jit_solution(7093131205028288897)
XLA Ops:
  0.0 42.8 %shard_map.37 = bf16[1,96,2048]{2,1,0:T(8,128)(2,1)} custom-call(bf16[1,96,2048]{2,1,0:T(8,128)(2,1)} %x_hbm.1, bf16[2048,16,2,128]{3,2,1,0:T(2,128)(2,1)} %bitcast.2, bf16[8,256,2048]{2,1,0:T(8,128)(2,1)} %bitcast.3), custom_call_target="tpu_custom_call" | custom-call | tf_op jit(solution)/shard_map/pallas_call | solution.py:263
  42.8 1.8 %copy.5 = bf16[1,96,2048]{2,1,0:T(8,128)(2,1)} copy(bf16[1,96,2048]{2,1,0:T(8,128)(2,1)} %shard_map.37) | data formatting | bytes 786432

commit v2 on v0

v2 whole, which is shorter than its diff:
```python
import functools
import math

import jax
import jax.numpy as jnp
from jax import lax
from jax.experimental import pallas as pl
from jax.experimental.pallas import tpu as pltpu
from jax.sharding import PartitionSpec as P

MESH = pl.DeviceIdType.MESH
F32 = jnp.float32
BF16 = jnp.bfloat16


def kernel(n, x_hbm, w_hbm, wo_hbm, y_ref,
           xbuf, xil, wstage, wo, kvout, qout, kvb, qb, acc, mrun, lrun, osend, orecv,
           sem_x, sem_w, sem_wo, sx_send, sx_recv, s_kv1, r_kv1, s_q1, r_q1,
           s_kv2, r_kv2, s_kv3, r_kv3, s_o, r_o):
    dp = lax.axis_index("dp")
    cy = lax.axis_index("cy")
    cx = lax.axis_index("cx")
    c = lax.axis_index("core")
    a = cx * (1 - c) + cy * c
    b = cy * (1 - c) + cx * c
    tok = xbuf.shape[1]
    dim = kvb.shape[-1]
    chip = 2 * tok
    width = xbuf.shape[2]
    npair = w_hbm.shape[1]
    nq, nkv = npair // 2, npair // 4
    own = nq // 2

    def xor(p, m):
        hi, lo = p // 2, p - p // 2 * 2
        hi = 1 - hi if m >= 2 else hi
        lo = 1 - lo if m % 2 else lo
        return 2 * hi + lo

    def at(ra, rb, core):
        return (dp, rb * (1 - c) + ra * c, ra * (1 - c) + rb * c, core)

    def remote(src, dst, ssem, rsem, device):
        return pltpu.make_async_remote_copy(
            src_ref=src, dst_ref=dst, send_sem=ssem, recv_sem=rsem, device_id=device, device_id_type=MESH)

    def recv(dst, sem):
        remote(dst, dst, s_kv1.at[0], sem, at(a, b, 1 - c)).wait_recv()

    def rows_of(p, size):
        return pl.ds(pl.multiple_of(p * size, size), size)

    x_cp = pltpu.make_async_copy(x_hbm.at[0], xbuf.at[c], sem_x)
    x_cp.start()
    far_a, far_b = 1 - a // 2, 1 - b // 2
    steps = [(c, far_a), (1 - c, far_b), (c, 1 - far_a), (1 - c, 1 - far_b)]
    pairs = []
    for plane, q in steps:
        pairs += [nq + own // 2 * plane + q, nq + nkv + own // 2 * plane + q]
    for q in (far_a, 1 - far_a):
        pairs += [own * c + 2 * q, own * c + 2 * q + 1]
    w_cps = [pltpu.make_async_copy(w_hbm.at[:, p], wstage.at[i], sem_w.at[i]) for i, p in enumerate(pairs)]

    def fetch(i):
        w_cps[2 * i].start()
        w_cps[2 * i + 1].start()

    fetch(0)

    barrier = pltpu.get_barrier_semaphore()
    peers = [at(a, b, 1 - c)]
    for m in range(1, n):
        for core in (c, 1 - c):
            peers += [at(xor(a, m), b, core), at(a, xor(b, m), core)]
    for p in peers:
        pl.semaphore_signal(barrier, inc=1, device_id=p, device_id_type=MESH)

    er = lax.broadcasted_iota(jnp.int32, (dim, 4 * dim), 0)
    ec = lax.broadcasted_iota(jnp.int32, (dim, 4 * dim), 1)
    sel = jnp.where(ec < 2 * dim, 2 * er, 2 * dim + 2 * er + 1)
    spread = jnp.where(ec == sel, 1.0, 0.0).astype(BF16)

    def expand(core):
        nb = width // dim
        step = 4
        for j0 in range(0, nb, step):
            xs = jnp.concatenate([xbuf[core, :, (j0 + j) * dim:(j0 + j + 1) * dim] for j in range(step)], axis=0)
            r = jnp.dot(xs, spread, preferred_element_type=F32).astype(BF16)
            for j in range(step):
                cols = slice((j0 + j) * 2 * dim, (j0 + j + 1) * 2 * dim)
                for e in range(2):
                    xil[e, core, :, cols] = r[j * tok:(j + 1) * tok, e * 2 * dim:(e + 1) * 2 * dim]

    def weights(i):
        w_cps[2 * i].wait()
        w_cps[2 * i + 1].wait()
        return jnp.concatenate([wstage[2 * i].reshape(2 * width, dim), wstage[2 * i + 1].reshape(2 * width, dim)], axis=1)

    sends = []

    def start(cp):
        cp.start()
        sends.append(cp)

    def kv_dot(i):
        r = jnp.dot(xil[:, c].reshape(chip, 2 * width), weights(i), preferred_element_type=F32).astype(BF16)
        for e in range(2):
            for kv in range(2):
                kvout[2 * i + e, kv] = r[e * tok:(e + 1) * tok, kv * dim:(kv + 1) * dim]

    def kv_send(i):
        own_plane, place = i % 2 == 0, (a, b)[i % 2]
        for low in range(2):
            m = low + (2 if i < 2 else 0)
            e = xor(place, m) - xor(place, m) // 2 * 2
            where = rows_of(2 * m + c, tok)
            if own_plane and m == 0:
                kvb[0, :, where] = kvout[2 * i + e]
                continue
            device = at(xor(a, m), b, c) if own_plane else at(a, xor(b, m), 1 - c)
            start(remote(kvout.at[2 * i + e], kvb.at[0, :, where], s_kv1.at[2 * i + low], r_kv1.at[m, c], device))

    def q_dot(i):
        r = jnp.dot(xil[...].reshape(2 * chip, 2 * width), weights(4 + i), preferred_element_type=F32).astype(BF16)
        for e in range(2):
            for h in range(2):
                qout[2 * i + e, h] = r[h * chip:(h + 1) * chip, e * dim:(e + 1) * dim]

    def q_send(i):
        for low in range(2):
            m = low + (2 if i == 0 else 0)
            e = xor(a, m) - xor(a, m) // 2 * 2
            if m == 0:
                qb[0] = qout[2 * i + e]
            else:
                start(remote(qout.at[2 * i + e], qb.at[m], s_q1.at[m], r_q1.at[m], at(xor(a, m), b, c)))

    def forward(m):
        for core in (c, 1 - c):
            if m > 0 or core is not c:
                recv(kvb.at[0, :, rows_of(2 * m + core, tok)], r_kv1.at[m, core])
        part = rows_of(m, chip)
        for v in (1, 3):
            start(remote(kvb.at[0, :, part], kvb.at[v, :, part], s_kv2.at[v, m], r_kv2.at[v, m], at(a, xor(b, v), c)))

    x_cp.wait()
    fetch(1)
    fetch(2)
    expand(c)
    kv_dot(0)
    fetch(3)
    pl.semaphore_wait(barrier, len(peers))
    x_rc = remote(xbuf.at[c], xbuf.at[c], sx_send, sx_recv, at(a, b, 1 - c))
    x_rc.start()
    kv_send(0)
    kv_dot(1)
    fetch(4)
    kv_send(1)
    kv_dot(2)
    fetch(5)
    kv_send(2)
    kv_dot(3)
    kv_send(3)
    heads = [own * c + xor(a, m) for m in range(n)] + [own * (1 - c) + xor(b, m) for m in range(n)]
    wo_cps = [pltpu.make_async_copy(wo_hbm.at[g], wo.at[k], sem_wo.at[k]) for k, g in enumerate(heads)]
    x_rc.wait_recv()
    expand(1 - c)
    q_dot(0)
    q_send(0)
    forward(2)
    forward(3)
    q_dot(1)
    q_send(1)
    for cp in wo_cps:
        cp.start()
    forward(1)
    forward(0)

    scale = dim ** -0.5 * math.log2(math.e)
    keys = kvb.shape[2]

    def attend(block, tiles, first, last, then):
        def scores(t):
            return lax.dot_general(qb[t].reshape(2 * chip, dim), kvb[block, 0], (((1,), (1,)), ((), ())),
                                   preferred_element_type=F32)

        def finish(t, p, alpha, l):
            o = jnp.dot(p, kvb[block, 1], preferred_element_type=F32)
            if not first:
                o = acc[t] * alpha + o
            if last:
                o = (o / jnp.sum(l, axis=1, keepdims=True)).astype(BF16)
                osend[t] = o.reshape(2, chip, dim)
                then(t)
            else:
                acc[t] = o

        ahead, held = scores(tiles[0]), None
        for k, t in enumerate(tiles):
            s = ahead
            if k + 1 < len(tiles):
                ahead = scores(tiles[k + 1])
            top = s[:, :dim]
            for j in range(1, keys // dim):
                top = jnp.maximum(top, s[:, j * dim:(j + 1) * dim])
            top = jnp.broadcast_to(jnp.max(top, axis=1, keepdims=True), (2 * chip, dim))
            alpha = None
            if not first:
                old = mrun[t]
                top = jnp.maximum(top, old)
                alpha = jnp.exp2((old - top) * scale)
            p, l = [], None
            for j in range(keys // dim):
                pj = jnp.exp2((s[:, j * dim:(j + 1) * dim] - top) * scale)
                l = pj if l is None else l + pj
                p.append(pj.astype(BF16))
            if not first:
                l = lrun[t] * alpha + l
            if not last:
                mrun[t] = top
                lrun[t] = l
            if held is not None:
                finish(*held)
            held = (t, jnp.concatenate(p, axis=1), alpha, l)
        finish(*held)

    def from_side(v, m):
        recv(kvb.at[v, :, rows_of(m, chip)], r_kv2.at[v, m])

    def relay(v, m):
        part = rows_of(m, chip)
        start(remote(kvb.at[v, :, part], kvb.at[2, :, part], s_kv3.at[m], r_kv3.at[m], at(a, xor(b, 4 - v), c)))

    attend(0, (0,), True, False, None)
    for m in (2, 3, 1):
        recv(qb.at[m], r_q1.at[m])
    from_side(1, 2)
    relay(1, 2)
    from_side(3, 3)
    relay(3, 3)
    attend(0, (1, 2, 3), True, False, None)
    for m in (3, 1, 0):
        from_side(1, m)
    relay(1, 1)
    for m in (2, 1, 0):
        from_side(3, m)
    relay(3, 0)
    attend(1, (0, 1, 2, 3), False, False, None)
    attend(3, (0, 1, 2, 3), False, False, None)
    for m in range(n):
        recv(kvb.at[2, :, rows_of(m, chip)], r_kv3.at[m])

    def give_back(m):
        for e, core in enumerate((c, 1 - c)):
            part = rows_of(core, tok)
            if m == 0 and e == 0:
                orecv[0] = osend[0, :, part]
            else:
                start(remote(osend.at[m, :, part], orecv.at[n * e + m], s_o.at[m, e], r_o.at[n * e + m],
                             at(xor(a, m), b, core)))

    attend(2, (2, 3, 1, 0), False, True, give_back)

    for cp in wo_cps:
        cp.wait()
    yacc = None
    for k in (0, n, 2, n + 2, 3, n + 3, 1, n + 1):
        if k > 0:
            recv(orecv.at[k], r_o.at[k])
        o = jnp.concatenate([orecv[k, 0], orecv[k, 1]], axis=1)
        r = jnp.dot(o, wo[k], preferred_element_type=F32)
        yacc = r if yacc is None else yacc + r
    y_ref[0] = yacc.astype(BF16)

    x_rc.wait_send()
    for cp in sends:
        cp.wait_send()


def solution(mesh):
    n = mesh.shape["cx"]
    assert mesh.shape["cy"] == n and n == 4 and mesh.shape["core"] == 2
    seq_spec = P("dp", ("cy", "cx", "core"))

    def local_layer(x_loc, w_qkv, w_out):
        _, tok, width = x_loc.shape
        heads, dim, out_width = w_out.shape
        all_heads = w_qkv.shape[1]
        kv = (all_heads - heads) // 2
        assert kv == 2 * n and heads == 2 * kv
        chip = 2 * tok
        keys = n * chip
        w_pairs = w_qkv.reshape(width, all_heads // 2, 2, dim)
        wo_pairs = w_out.reshape(kv, 2 * dim, out_width)
        dma = pltpu.SemaphoreType.DMA
        return pl.pallas_call(
            functools.partial(kernel, n),
            out_shape=pltpu.VMEM(x_loc.shape, BF16),
            in_specs=[pl.BlockSpec(memory_space=pl.ANY)] * 3,
            out_specs=pl.BlockSpec(memory_space=pltpu.VMEM),
            scratch_shapes=[
                pltpu.VMEM((2, tok, width), BF16),
                pltpu.VMEM((2, 2, tok, 2 * width), BF16),
                pltpu.VMEM((kv + n, width, 2, dim), BF16),
                pltpu.VMEM((kv, 2 * dim, out_width), BF16),
                pltpu.VMEM((kv, 2, tok, dim), BF16),
                pltpu.VMEM((n, 2, chip, dim), BF16),
                pltpu.VMEM((4, 2, keys, dim), BF16),
                pltpu.VMEM((n, 2, chip, dim), BF16),
                pltpu.VMEM((n, 2 * chip, dim), F32),
                pltpu.VMEM((n, 2 * chip, dim), F32),
                pltpu.VMEM((n, 2 * chip, dim), F32),
                pltpu.VMEM((n, 2, chip, dim), BF16),
                pltpu.VMEM((kv, 2, tok, dim), BF16),
                dma, dma((kv + n,)), dma((kv,)),
                dma, dma,
                dma((kv,)), dma((n, 2)), dma((n,)), dma((n,)),
                dma((n, n)), dma((n, n)), dma((n,)), dma((n,)),
                dma((n, 2)), dma((kv,)),
            ],
            compiler_params=pltpu.CompilerParams(
                collective_id=0, has_side_effects=True, vmem_limit_bytes=58 * 1024 * 1024),
        )(x_loc, w_pairs, wo_pairs)

    return jax.shard_map(local_layer, mesh=mesh, in_specs=(seq_spec, P(), P()), out_specs=seq_spec, check_vma=False)
```

time: 105 us -> 36.8 us (0.35)
  blocking collectives: 37.9 us -> 0 us
  Pallas kernels: 0 us -> 35.9 us
  waiting for transfers between devices: 24.4 us -> 0 us
  matrix products: 22.4 us -> 0 us
  between operations: 13.6 us -> 0.01 us
  other arithmetic: 3.26 us -> 0 us
  local copies, waits for them, and re-layouts: 2.83 us -> 0.75 us
    all_to_all x4 -> x0, blocking collectives: 37.9 us -> none  [the longest x1 16.3 us: local_layer(): packed = lax.all_to_all(packed, 'cx', 1, 0, tiled=True)]
    pallas_call x0 -> x1, Pallas kernels: none -> 35.9 us  [local_layer(): pl.pallas_call(functools.partial(kernel, n), out_shape=pltpu.VMEM(x_loc.s...]
    all_gather x1 -> x0, waiting for transfers between devices: 24.3 us -> none  [local_layer(): kv_all = lax.all_gather(packed[:, 0, q_local:], 'cy')]
    dot_general x10 -> x0, matrix products: 22.4 us -> none  [the longest x1 11.3 us: local_layer(): jnp.einsum('sc,chd->shd', x_loc[0], w_qkv, preferred_element_type=jnp.flo...]
    reduce_sum x2 -> x0, other arithmetic: 3.12 us -> none  [local_layer(): run_sum = run_sum * rescale + weights.sum(axis=-1)]
  transfers between devices with their start and end apart: 1 -> 0, of which waited for: 1 -> 0; matrix products, arithmetic and copies ran while one was open for 0% -> 0% of each run, Pallas kernels for 0% -> 0%
where the time goes in v2:
time: 36.8 us; the launch traced here: 36.7 us
  Pallas kernels  35.9 us (98%)
  local copies, waits for them, and re-layouts  0.75 us (2%)
    pallas_call x1, Pallas kernels, local_layer(): pl.pallas_call(functools.partial(kernel, n), out_shape=pltpu.VMEM(x_loc.s...  35.9 us
    unnamed x1, local copies, waits for them, and re-layouts  0.75 us

profile of v2, /device:TPU:97, one launch (start us, length us, event | category | flops | bytes accessed | tf_op | source)
XLA Modules:
  0.0 36.7 jit_solution(14862399045081565526)
XLA Ops:
  0.0 35.9 %shard_map.37 = bf16[1,96,2048]{2,1,0:T(8,128)(2,1)S(1)} custom-call(bf16[1,96,2048]{2,1,0:T(8,128)(2,1)} %x_hbm.1, bf16[2048,16,2,128]{3,2,1,0:T(2,128)(2,1)} %bitcast.2, bf16[8,256,2048]{2,1,0:T(8,128)(2,1)} %bitcast.3), custom_call_target="tpu_custom_call" | custom-call | tf_op jit(solution)/shard_map/pallas_call | solution.py:296
  35.9 0.7 %copy.5 = bf16[1,96,2048]{2,1,0:T(8,128)(2,1)} copy(bf16[1,96,2048]{2,1,0:T(8,128)(2,1)S(1)} %shard_map.37) | data formatting | bytes 786432

commit v3 on v2

--- a/solution.py
+++ b/solution.py
@@ -75,21 +75,21 @@
     for p in peers:
         pl.semaphore_signal(barrier, inc=1, device_id=p, device_id_type=MESH)
 
-    er = lax.broadcasted_iota(jnp.int32, (dim, 4 * dim), 0)
-    ec = lax.broadcasted_iota(jnp.int32, (dim, 4 * dim), 1)
-    sel = jnp.where(ec < 2 * dim, 2 * er, 2 * dim + 2 * er + 1)
-    spread = jnp.where(ec == sel, 1.0, 0.0).astype(BF16)
+    lanes = 2 * dim
+    copy = jnp.where(lax.broadcasted_iota(jnp.int32, (dim, lanes), 1) // 2
+                     == lax.broadcasted_iota(jnp.int32, (dim, lanes), 0), 1.0, 0.0).astype(BF16)
+    odd = lax.rem(lax.broadcasted_iota(jnp.int32, (tok, lanes), 1), 2)
+    keep = [jnp.where(odd == e, 1.0, 0.0).astype(BF16) for e in range(2)]
 
     def expand(core):
-        nb = width // dim
         step = 4
-        for j0 in range(0, nb, step):
+        for j0 in range(0, width // dim, step):
             xs = jnp.concatenate([xbuf[core, :, (j0 + j) * dim:(j0 + j + 1) * dim] for j in range(step)], axis=0)
-            r = jnp.dot(xs, spread, preferred_element_type=F32).astype(BF16)
+            r = jnp.dot(xs, copy, preferred_element_type=F32).astype(BF16)
             for j in range(step):
-                cols = slice((j0 + j) * 2 * dim, (j0 + j + 1) * 2 * dim)
                 for e in range(2):
-                    xil[e, core, :, cols] = r[j * tok:(j + 1) * tok, e * 2 * dim:(e + 1) * 2 * dim]
+                    xil[rows_of(2 * e + core, tok), (j0 + j) * lanes:(j0 + j + 1) * lanes] = \
+                        r[j * tok:(j + 1) * tok] * keep[e]
 
     def weights(i):
         w_cps[2 * i].wait()
@@ -103,7 +103,8 @@
         sends.append(cp)
 
     def kv_dot(i):
-        r = jnp.dot(xil[:, c].reshape(chip, 2 * width), weights(i), preferred_element_type=F32).astype(BF16)
+        rows = jnp.concatenate([xil[rows_of(c, tok)], xil[rows_of(2 + c, tok)]], axis=0)
+        r = jnp.dot(rows, weights(i), preferred_element_type=F32).astype(BF16)
         for e in range(2):
             for kv in range(2):
                 kvout[2 * i + e, kv] = r[e * tok:(e + 1) * tok, kv * dim:(kv + 1) * dim]
@@ -121,10 +122,11 @@
             start(remote(kvout.at[2 * i + e], kvb.at[0, :, where], s_kv1.at[2 * i + low], r_kv1.at[m, c], device))
 
     def q_dot(i):
-        r = jnp.dot(xil[...].reshape(2 * chip, 2 * width), weights(4 + i), preferred_element_type=F32).astype(BF16)
-        for e in range(2):
-            for h in range(2):
-                qout[2 * i + e, h] = r[h * chip:(h + 1) * chip, e * dim:(e + 1) * dim]
+        w = weights(4 + i)
+        for h in range(2):
+            r = jnp.dot(xil[h * chip:(h + 1) * chip], w, preferred_element_type=F32).astype(BF16)
+            for e in range(2):
+                qout[2 * i + e, h] = r[:, e * dim:(e + 1) * dim]
 
     def q_send(i):
         for low in range(2):
@@ -150,8 +152,10 @@
     kv_dot(0)
     fetch(3)
     pl.semaphore_wait(barrier, len(peers))
-    x_rc = remote(xbuf.at[c], xbuf.at[c], sx_send, sx_recv, at(a, b, 1 - c))
-    x_rc.start()
+    x_rcs = [remote(xil.at[rows_of(2 * e + c, tok)], xil.at[rows_of(2 * e + c, tok)], sx_send.at[e], sx_recv.at[e],
+                    at(a, b, 1 - c)) for e in range(2)]
+    for cp in x_rcs:
+        start(cp)
     kv_send(0)
     kv_dot(1)
     fetch(4)
@@ -163,49 +167,55 @@
     kv_send(3)
     heads = [own * c + xor(a, m) for m in range(n)] + [own * (1 - c) + xor(b, m) for m in range(n)]
     wo_cps = [pltpu.make_async_copy(wo_hbm.at[g], wo.at[k], sem_wo.at[k]) for k, g in enumerate(heads)]
-    x_rc.wait_recv()
-    expand(1 - c)
+    for cp in x_rcs:
+        cp.wait_recv()
     q_dot(0)
     q_send(0)
-    forward(2)
-    forward(3)
     q_dot(1)
     q_send(1)
     for cp in wo_cps:
         cp.start()
+    forward(2)
+    forward(3)
     forward(1)
     forward(0)
 
     scale = dim ** -0.5 * math.log2(math.e)
     keys = kvb.shape[2]
 
-    def attend(block, tiles, first, last, then):
-        def scores(t):
-            return lax.dot_general(qb[t].reshape(2 * chip, dim), kvb[block, 0], (((1,), (1,)), ((), ())),
+    def attend(items, then):
+        def part(group, kv):
+            if group in (0, 3):
+                return kvb[0 if group == 0 else 2, kv]
+            rows = slice(keys // 2, keys) if group == 1 else slice(0, keys // 2)
+            return jnp.concatenate([kvb[1, kv, rows], kvb[3, kv, rows]], axis=0)
+
+        def scores(group, t):
+            return lax.dot_general(qb[t].reshape(2 * chip, dim), part(group, 0), (((1,), (1,)), ((), ())),
                                    preferred_element_type=F32)
 
-        def finish(t, p, alpha, l):
-            o = jnp.dot(p, kvb[block, 1], preferred_element_type=F32)
-            if not first:
+        def finish(group, t, p, alpha, l):
+            o = jnp.dot(p, part(group, 1), preferred_element_type=F32)
+            if group != 0:
                 o = acc[t] * alpha + o
-            if last:
+            if group == 3:
                 o = (o / jnp.sum(l, axis=1, keepdims=True)).astype(BF16)
                 osend[t] = o.reshape(2, chip, dim)
                 then(t)
             else:
                 acc[t] = o
 
-        ahead, held = scores(tiles[0]), None
-        for k, t in enumerate(tiles):
+        ahead, held = scores(*items[0]), None
+        for k, (group, t) in enumerate(items):
             s = ahead
-            if k + 1 < len(tiles):
-                ahead = scores(tiles[k + 1])
+            if k + 1 < len(items):
+                ahead = scores(*items[k + 1])
             top = s[:, :dim]
             for j in range(1, keys // dim):
                 top = jnp.maximum(top, s[:, j * dim:(j + 1) * dim])
             top = jnp.broadcast_to(jnp.max(top, axis=1, keepdims=True), (2 * chip, dim))
             alpha = None
-            if not first:
+            if group != 0:
                 old = mrun[t]
                 top = jnp.maximum(top, old)
                 alpha = jnp.exp2((old - top) * scale)
@@ -214,14 +224,14 @@
                 pj = jnp.exp2((s[:, j * dim:(j + 1) * dim] - top) * scale)
                 l = pj if l is None else l + pj
                 p.append(pj.astype(BF16))
-            if not first:
+            if group != 0:
                 l = lrun[t] * alpha + l
-            if not last:
+            if group != 3:
                 mrun[t] = top
                 lrun[t] = l
             if held is not None:
                 finish(*held)
-            held = (t, jnp.concatenate(p, axis=1), alpha, l)
+            held = (group, t, jnp.concatenate(p, axis=1), alpha, l)
         finish(*held)
 
     def from_side(v, m):
@@ -231,22 +241,23 @@
         part = rows_of(m, chip)
         start(remote(kvb.at[v, :, part], kvb.at[2, :, part], s_kv3.at[m], r_kv3.at[m], at(a, xor(b, 4 - v), c)))
 
-    attend(0, (0,), True, False, None)
+    attend([(0, 0)], None)
+    for v, m in ((1, 2), (3, 3)):
+        from_side(v, m)
+        relay(v, m)
+    for v, m in ((1, 3), (3, 2)):
+        from_side(v, m)
+    attend([(1, 0)], None)
     for m in (2, 3, 1):
         recv(qb.at[m], r_q1.at[m])
-    from_side(1, 2)
-    relay(1, 2)
-    from_side(3, 3)
-    relay(3, 3)
-    attend(0, (1, 2, 3), True, False, None)
-    for m in (3, 1, 0):
-        from_side(1, m)
-    relay(1, 1)
-    for m in (2, 1, 0):
-        from_side(3, m)
-    relay(3, 0)
-    attend(1, (0, 1, 2, 3), False, False, None)
-    attend(3, (0, 1, 2, 3), False, False, None)
+    attend([(0, 1), (0, 2), (0, 3), (1, 1)], None)
+    for v, m in ((1, 1), (3, 0)):
+        from_side(v, m)
+        relay(v, m)
+    attend([(1, 2), (1, 3)], None)
+    for v, m in ((1, 0), (3, 1)):
+        from_side(v, m)
+    attend([(2, t) for t in range(n)], None)
     for m in range(n):
         recv(kvb.at[2, :, rows_of(m, chip)], r_kv3.at[m])
 
@@ -259,12 +270,12 @@
                 start(remote(osend.at[m, :, part], orecv.at[n * e + m], s_o.at[m, e], r_o.at[n * e + m],
                              at(xor(a, m), b, core)))
 
-    attend(2, (2, 3, 1, 0), False, True, give_back)
+    attend([(3, 2), (3, 3), (3, 1), (3, 0)], give_back)
 
     for cp in wo_cps:
         cp.wait()
     yacc = None
-    for k in (0, n, 2, n + 2, 3, n + 3, 1, n + 1):
+    for k in (0, 2, n + 2, 3, n + 3, n, 1, n + 1):
         if k > 0:
             recv(orecv.at[k], r_o.at[k])
         o = jnp.concatenate([orecv[k, 0], orecv[k, 1]], axis=1)
@@ -272,7 +283,6 @@
         yacc = r if yacc is None else yacc + r
     y_ref[0] = yacc.astype(BF16)
 
-    x_rc.wait_send()
     for cp in sends:
         cp.wait_send()
 
@@ -300,7 +310,7 @@
             out_specs=pl.BlockSpec(memory_space=pltpu.VMEM),
             scratch_shapes=[
                 pltpu.VMEM((2, tok, width), BF16),
-                pltpu.VMEM((2, 2, tok, 2 * width), BF16),
+                pltpu.VMEM((2 * chip, 2 * width), BF16),
                 pltpu.VMEM((kv + n, width, 2, dim), BF16),
                 pltpu.VMEM((kv, 2 * dim, out_width), BF16),
                 pltpu.VMEM((kv, 2, tok, dim), BF16),
@@ -313,7 +323,7 @@
                 pltpu.VMEM((n, 2, chip, dim), BF16),
                 pltpu.VMEM((kv, 2, tok, dim), BF16),
                 dma, dma((kv + n,)), dma((kv,)),
-                dma, dma,
+                dma((2,)), dma((2,)),
                 dma((kv,)), dma((n, 2)), dma((n,)), dma((n,)),
                 dma((n, n)), dma((n, n)), dma((n,)), dma((n,)),
                 dma((n, 2)), dma((kv,)),

time: 36.8 us -> 34.9 us (0.948)
  Pallas kernels: 35.9 us -> 34 us
    pallas_call x1, Pallas kernels: 35.9 us -> 34 us  [local_layer(): pl.pallas_call(functools.partial(kernel, n), out_shape=pltpu.VMEM(x_loc.s...]
where the time goes in v3:
time: 34.9 us; the launch traced here: 34.8 us
  Pallas kernels  34 us (97%)
  local copies, waits for them, and re-layouts  0.75 us (2%)
    pallas_call x1, Pallas kernels, local_layer(): pl.pallas_call(functools.partial(kernel, n), out_shape=pltpu.VMEM(x_loc.s...  34 us
    unnamed x1, local copies, waits for them, and re-layouts  0.75 us

profile of v3, /device:TPU:97, one launch (start us, length us, event | category | flops | bytes accessed | tf_op | source)
XLA Modules:
  0.0 34.8 jit_solution(11267397025711581057)
XLA Ops:
  0.0 34.0 %shard_map.37 = bf16[1,96,2048]{2,1,0:T(8,128)(2,1)S(1)} custom-call(bf16[1,96,2048]{2,1,0:T(8,128)(2,1)} %x_hbm.1, bf16[2048,16,2,128]{3,2,1,0:T(2,128)(2,1)} %bitcast.2, bf16[8,256,2048]{2,1,0:T(8,128)(2,1)} %bitcast.3), custom_call_target="tpu_custom_call" | custom-call | tf_op jit(solution)/shard_map/pallas_call | solution.py:306
  34.0 0.7 %copy.5 = bf16[1,96,2048]{2,1,0:T(8,128)(2,1)} copy(bf16[1,96,2048]{2,1,0:T(8,128)(2,1)S(1)} %shard_map.37) | data formatting | bytes 786432

commit v4 on v3

--- a/solution.py
+++ b/solution.py
@@ -16,7 +16,7 @@
 def kernel(n, x_hbm, w_hbm, wo_hbm, y_ref,
            xbuf, xil, wstage, wo, kvout, qout, kvb, qb, acc, mrun, lrun, osend, orecv,
            sem_x, sem_w, sem_wo, sx_send, sx_recv, s_kv1, r_kv1, s_q1, r_q1,
-           s_kv2, r_kv2, s_kv3, r_kv3, s_o, r_o):
+           s_kv2, r_kv2, s_kv3, s_o, r_o):
     dp = lax.axis_index("dp")
     cy = lax.axis_index("cy")
     cx = lax.axis_index("cx")
@@ -50,6 +50,11 @@
     def rows_of(p, size):
         return pl.ds(pl.multiple_of(p * size, size), size)
 
+    turn = {0: 0, 2: 1, 3: 2, 1: 3}
+
+    def spot(m):
+        return pl.ds(turn[m] * chip, chip)
+
     x_cp = pltpu.make_async_copy(x_hbm.at[0], xbuf.at[c], sem_x)
     x_cp.start()
     far_a, far_b = 1 - a // 2, 1 - b // 2
@@ -114,7 +119,7 @@
         for low in range(2):
             m = low + (2 if i < 2 else 0)
             e = xor(place, m) - xor(place, m) // 2 * 2
-            where = rows_of(2 * m + c, tok)
+            where = rows_of(2 * turn[m] + c, tok)
             if own_plane and m == 0:
                 kvb[0, :, where] = kvout[2 * i + e]
                 continue
@@ -137,13 +142,16 @@
             else:
                 start(remote(qout.at[2 * i + e], qb.at[m], s_q1.at[m], r_q1.at[m], at(xor(a, m), b, c)))
 
+    def onward(m, v):
+        part = spot(m)
+        start(remote(kvb.at[0, :, part], kvb.at[v, :, part], s_kv2.at[v, m], r_kv2.at[v, m], at(a, xor(b, v), c)))
+
     def forward(m):
         for core in (c, 1 - c):
             if m > 0 or core is not c:
-                recv(kvb.at[0, :, rows_of(2 * m + core, tok)], r_kv1.at[m, core])
-        part = rows_of(m, chip)
-        for v in (1, 3):
-            start(remote(kvb.at[0, :, part], kvb.at[v, :, part], s_kv2.at[v, m], r_kv2.at[v, m], at(a, xor(b, v), c)))
+                recv(kvb.at[0, :, rows_of(2 * turn[m] + core, tok)], r_kv1.at[m, core])
+        onward(m, 1)
+        onward(m, 3)
 
     x_cp.wait()
     fetch(1)
@@ -171,6 +179,7 @@
         cp.wait_recv()
     q_dot(0)
     q_send(0)
+    forward(0)
     q_dot(1)
     q_send(1)
     for cp in wo_cps:
@@ -178,7 +187,8 @@
     forward(2)
     forward(3)
     forward(1)
-    forward(0)
+    onward(3, 2)
+    onward(1, 2)
 
     scale = dim ** -0.5 * math.log2(math.e)
     keys = kvb.shape[2]
@@ -187,7 +197,7 @@
         def part(group, kv):
             if group in (0, 3):
                 return kvb[0 if group == 0 else 2, kv]
-            rows = slice(keys // 2, keys) if group == 1 else slice(0, keys // 2)
+            rows = slice(0, keys // 2) if group == 1 else slice(keys // 2, keys)
             return jnp.concatenate([kvb[1, kv, rows], kvb[3, kv, rows]], axis=0)
 
         def scores(group, t):
@@ -235,31 +245,28 @@
         finish(*held)
 
     def from_side(v, m):
-        recv(kvb.at[v, :, rows_of(m, chip)], r_kv2.at[v, m])
+        recv(kvb.at[v, :, spot(m)], r_kv2.at[v, m])
 
     def relay(v, m):
-        part = rows_of(m, chip)
-        start(remote(kvb.at[v, :, part], kvb.at[2, :, part], s_kv3.at[m], r_kv3.at[m], at(a, xor(b, 4 - v), c)))
+        part = spot(m)
+        start(remote(kvb.at[v, :, part], kvb.at[2, :, part], s_kv3.at[m], r_kv2.at[2, m], at(a, xor(b, 4 - v), c)))
 
     attend([(0, 0)], None)
-    for v, m in ((1, 2), (3, 3)):
-        from_side(v, m)
-        relay(v, m)
-    for v, m in ((1, 3), (3, 2)):
-        from_side(v, m)
-    attend([(1, 0)], None)
+    from_side(1, 0)
+    relay(1, 0)
     for m in (2, 3, 1):
         recv(qb.at[m], r_q1.at[m])
-    attend([(0, 1), (0, 2), (0, 3), (1, 1)], None)
-    for v, m in ((1, 1), (3, 0)):
-        from_side(v, m)
-        relay(v, m)
-    attend([(1, 2), (1, 3)], None)
-    for v, m in ((1, 0), (3, 1)):
+    attend([(0, 1), (0, 2), (0, 3)], None)
+    from_side(3, 2)
+    relay(3, 2)
+    from_side(1, 2)
+    from_side(3, 0)
+    attend([(1, t) for t in range(n)], None)
+    for v, m in ((1, 3), (3, 3), (1, 1), (3, 1)):
         from_side(v, m)
     attend([(2, t) for t in range(n)], None)
-    for m in range(n):
-        recv(kvb.at[2, :, rows_of(m, chip)], r_kv3.at[m])
+    for m in (0, 2, 3, 1):
+        from_side(2, m)
 
     def give_back(m):
         for e, core in enumerate((c, 1 - c)):
@@ -275,7 +282,7 @@
     for cp in wo_cps:
         cp.wait()
     yacc = None
-    for k in (0, 2, n + 2, 3, n + 3, n, 1, n + 1):
+    for k in (0, n, 1, 3, 2, n + 1, n + 3, n + 2):
         if k > 0:
             recv(orecv.at[k], r_o.at[k])
         o = jnp.concatenate([orecv[k, 0], orecv[k, 1]], axis=1)
@@ -325,7 +332,7 @@
                 dma, dma((kv + n,)), dma((kv,)),
                 dma((2,)), dma((2,)),
                 dma((kv,)), dma((n, 2)), dma((n,)), dma((n,)),
-                dma((n, n)), dma((n, n)), dma((n,)), dma((n,)),
+                dma((n, n)), dma((n, n)), dma((n,)),
                 dma((n, 2)), dma((kv,)),
             ],
             compiler_params=pltpu.CompilerParams(

time: 34.9 us -> 33.5 us (0.960)
  Pallas kernels: 34 us -> 32.6 us
    pallas_call x1, Pallas kernels: 34 us -> 32.6 us  [local_layer(): pl.pallas_call(functools.partial(kernel, n), out_shape=pltpu.VMEM(x_loc.s...]
where the time goes in v4:
time: 33.5 us; the launch traced here: 33.4 us
  Pallas kernels  32.6 us (97%)
  local copies, waits for them, and re-layouts  0.75 us (2%)
    pallas_call x1, Pallas kernels, local_layer(): pl.pallas_call(functools.partial(kernel, n), out_shape=pltpu.VMEM(x_loc.s...  32.6 us
    unnamed x1, local copies, waits for them, and re-layouts  0.75 us

profile of v4, /device:TPU:97, one launch (start us, length us, event | category | flops | bytes accessed | tf_op | source)
XLA Modules:
  0.0 33.4 jit_solution(7184687430793244894)
XLA Ops:
  0.0 32.6 %shard_map.37 = bf16[1,96,2048]{2,1,0:T(8,128)(2,1)S(1)} custom-call(bf16[1,96,2048]{2,1,0:T(8,128)(2,1)} %x_hbm.1, bf16[2048,16,2,128]{3,2,1,0:T(2,128)(2,1)} %bitcast.2, bf16[8,256,2048]{2,1,0:T(8,128)(2,1)} %bitcast.3), custom_call_target="tpu_custom_call" | custom-call | tf_op jit(solution)/shard_map/pallas_call | solution.py:313
  32.6 0.7 %copy.5 = bf16[1,96,2048]{2,1,0:T(8,128)(2,1)} copy(bf16[1,96,2048]{2,1,0:T(8,128)(2,1)S(1)} %shard_map.37) | data formatting | bytes 786432

commit v5 on v4

--- a/solution.py
+++ b/solution.py
@@ -277,12 +277,12 @@
                 start(remote(osend.at[m, :, part], orecv.at[n * e + m], s_o.at[m, e], r_o.at[n * e + m],
                              at(xor(a, m), b, core)))
 
-    attend([(3, 2), (3, 3), (3, 1), (3, 0)], give_back)
+    attend([(3, 3), (3, 2), (3, 1), (3, 0)], give_back)
 
     for cp in wo_cps:
         cp.wait()
     yacc = None
-    for k in (0, n, 1, 3, 2, n + 1, n + 3, n + 2):
+    for k in (0, n, 1, 2, n + 1, n + 2, 3, n + 3):
         if k > 0:
             recv(orecv.at[k], r_o.at[k])
         o = jnp.concatenate([orecv[k, 0], orecv[k, 1]], axis=1)

time: 33.5 us -> 33.2 us (level)
  no operation moved by 1% of the time
where the time goes in v5:
time: 33.2 us; the launch traced here: 33.1 us
  Pallas kernels  32.3 us (97%)
  local copies, waits for them, and re-layouts  0.75 us (2%)
    pallas_call x1, Pallas kernels, local_layer(): pl.pallas_call(functools.partial(kernel, n), out_shape=pltpu.VMEM(x_loc.s...  32.3 us
    unnamed x1, local copies, waits for them, and re-layouts  0.75 us

profile of v5, /device:TPU:97, one launch (start us, length us, event | category | flops | bytes accessed | tf_op | source)
XLA Modules:
  0.0 33.1 jit_solution(15782092385958330344)
XLA Ops:
  0.0 32.3 %shard_map.37 = bf16[1,96,2048]{2,1,0:T(8,128)(2,1)S(1)} custom-call(bf16[1,96,2048]{2,1,0:T(8,128)(2,1)} %x_hbm.1, bf16[2048,16,2,128]{3,2,1,0:T(2,128)(2,1)} %bitcast.2, bf16[8,256,2048]{2,1,0:T(8,128)(2,1)} %bitcast.3), custom_call_target="tpu_custom_call" | custom-call | tf_op jit(solution)/shard_map/pallas_call | solution.py:313
  32.3 0.7 %copy.5 = bf16[1,96,2048]{2,1,0:T(8,128)(2,1)} copy(bf16[1,96,2048]{2,1,0:T(8,128)(2,1)S(1)} %shard_map.37) | data formatting | bytes 786432
